TPU v7x, 32 devices: a whole 2x2x4 slice. The times are simulated.
32 devices in a mesh: shard: 4 (over y, x), context: 2 (over core), tensor: 4 (over z).
Axes of the slice: x: 2, y: 2, z: 4, core: 2. Of those that a mesh axis runs over, the one named last changes fastest.
Arguments:
- inputs: bfloat16 [4, 1024, 1024], P('shard', 'context'), may hold values from -6 to 6
- cotangent: bfloat16 [4, 1024, 1024], P('shard', 'context'), may hold values from -6 to 6
- segments: int32 [4, 1024], P('shard'), may hold values from 0 to 3, never falling along the last dimension, each value on 1 to 800 neighbouring positions
- buckets: int32 [2047], replicated, may hold values from 0 to 511, as said below
- w_query: bfloat16 [1024, 1024], P(('shard', 'context'), 'tensor'), may hold values from -0.1875 to 0.1875
- w_key: bfloat16 [1024, 1024], P(('shard', 'context'), 'tensor'), may hold values from -0.1875 to 0.1875
- w_value: bfloat16 [1024, 1024], P(('shard', 'context'), 'tensor'), may hold values from -0.1875 to 0.1875
- w_output: bfloat16 [1024, 1024], P('tensor', ('shard', 'context')), may hold values from -3 to 3
- w_up: bfloat16 [1024, 4096], P(('shard', 'context'), 'tensor'), may hold values from -0.1875 to 0.1875
- w_down: bfloat16 [4096, 1024], P('tensor', ('shard', 'context')), may hold values from -0.09375 to 0.09375
- positions: bfloat16 [512, 1024], P(None, ('shard', 'context')), may hold values from -6 to 6
- gain_attn: bfloat16 [1024], P(('shard', 'context')), may hold values from 0.5 to 1.5
- bias_attn: bfloat16 [1024], P(('shard', 'context')), may hold values from -4 to 4
- gain_ffn: bfloat16 [1024], P(('shard', 'context')), may hold values from 0.5 to 1.5
- bias_ffn: bfloat16 [1024], P(('shard', 'context')), may hold values from -4 to 4
Outputs:
- outputs: bfloat16 [4, 1024, 1024], P('shard', 'context')
- grad_inputs: bfloat16 [4, 1024, 1024], P('shard', 'context')
- grad_query: float32 [1024, 1024], P(('shard', 'context'), 'tensor')
- grad_key: float32 [1024, 1024], P(('shard', 'context'), 'tensor')
- grad_value: float32 [1024, 1024], P(('shard', 'context'), 'tensor')
- grad_output: float32 [1024, 1024], P('tensor', ('shard', 'context'))
- grad_up: float32 [1024, 4096], P(('shard', 'context'), 'tensor')
- grad_down: float32 [4096, 1024], P('tensor', ('shard', 'context'))
- grad_positions: float32 [512, 1024], P(None, ('shard', 'context'))
- grad_gain_attn: float32 [1024], P(('shard', 'context'))
- grad_bias_attn: float32 [1024], P(('shard', 'context'))
- grad_gain_ffn: float32 [1024], P(('shard', 'context'))
- grad_bias_ffn: float32 [1024], P(('shard', 'context'))
Inputs may be any that keep to these rules, and one draw needn't show every extreme that they name: buckets[d + 1023] is the bucket of the distance d from key to query; it is 256 at d = 0, never falls as d rises, and equals d + 256 for small distances. `segments`: within a sequence document numbers never fall; each document has at least one token.
All inputs are finite; a program needn't handle non-finite values.
Results may differ from a plain program's by a relative error of at most 0.02.
Values may be sent and summed in bfloat16 or wider, within the bound.
A program may use at most 192 MiB of HBM per device.

v0:
```python
import functools
import math
from functools import partial
import jax, jax.numpy as jnp
from jax import lax
from jax.experimental import pallas as pl
from jax.experimental.pallas import tpu as pltpu
HD=64
NEG=-1000000000.0
TILE=128
F32=jnp.float32
BF=jnp.bfloat16

def dotf(a,b,ca,cb,precision=None):
    return lax.dot_general(a,b,(((ca,),(cb,)),((),())),preferred_element_type=F32,precision=precision)

def reversal(n,dtype):
    r=lax.broadcasted_iota(jnp.int32,(n,n),0); c=lax.broadcasted_iota(jnp.int32,(n,n),1)
    return (r+c==n-1).astype(F32).astype(dtype)

def attend_kernel(q_ref,k_ref,v_ref,kd_ref,pq_ref,sq_ref,sk_ref,ctx_ref,p_ref,st_ref,*,scale):
    rows=q_ref.shape[1]; total=k_ref.shape[1]; tile=min(TILE,rows)
    same_row=sk_ref[0]
    for half in range(2):
        cols=slice(half*HD,(half+1)*HD)
        q=q_ref[0][:,cols]; k=k_ref[0][:,cols]; v=v_ref[0][:,cols]
        kd=kd_ref[:,cols]; pq=pq_ref[:,cols]
        for j0 in range(0,total,TILE):
            width=rows+TILE; start=total-j0-TILE
            b=dotf(k[j0:j0+TILE],pq[start:start+width],1,1)
            b=pltpu.roll(b,width-TILE+1,axis=1,stride=1,stride_axis=0)[:,:rows]
            st_ref[:,j0:j0+TILE]=b.T
        for i0 in range(0,rows,tile):
            width=total+tile; start=rows-i0-tile
            qt=q[i0:i0+tile]
            a=dotf(qt,kd[start:start+width],1,1)
            a=pltpu.roll(a,width-tile+1,axis=1,stride=1,stride_axis=0)[:,:total]
            raw=dotf(qt,k,1,1)+a+st_ref[i0:i0+tile,:]
            s=jnp.where(sq_ref[0][i0:i0+tile]==same_row,raw*scale,NEG)
            e=jnp.exp(s-jnp.max(s,axis=1,keepdims=True))
            p=e*(1.0/jnp.sum(e,axis=1,keepdims=True))
            p_ref[0,half,i0:i0+tile,:]=p
            ctx_ref[0,i0:i0+tile,cols]=dotf(p.astype(BF),v,1,0).astype(BF)

def attend_back_kernel(q_ref,k_ref,v_ref,kd_ref,pq_ref,p_ref,dc_ref,dq_ref,dk_ref,dv_ref,dkd_ref,dpq_ref,ds_ref,pl_ref,dkt_ref,*,scale,between=None):
    rows=q_ref.shape[1]; total=k_ref.shape[1]; tile=min(TILE,rows)
    @pl.when(pl.program_id(1)==0)
    def _():
        dkd_ref[...]=jnp.zeros_like(dkd_ref)
        dpq_ref[...]=jnp.zeros_like(dpq_ref)
    flip_t=reversal(tile,BF); flip_j=reversal(TILE,BF)
    hi=lax.Precision.HIGHEST
    for half in range(2):
        cols=slice(half*HD,(half+1)*HD)
        q=q_ref[0][:,cols]; k=k_ref[0][:,cols]; v=v_ref[0][:,cols]; dc=dc_ref[0][:,cols]
        kd=kd_ref[:,cols]; pq=pq_ref[:,cols]
        for i0 in range(0,rows,tile):
            width=total+tile; start=rows-i0-tile
            p=p_ref[0,half,i0:i0+tile,:]
            dp=dotf(dc[i0:i0+tile],v,1,1)
            inner=jnp.sum(p*dp,axis=1,keepdims=True)
            ds=(p*(dp-inner)*scale).astype(BF)
            ds_ref[i0:i0+tile,:]=ds
            pl_ref[i0:i0+tile,:]=p.astype(BF)
            rev=dotf(flip_t,ds,1,0).astype(BF)
            rev=jnp.concatenate([rev,jnp.zeros((tile,tile),BF)],axis=1)
            rev=pltpu.roll(rev,0,axis=1,stride=1,stride_axis=0)
            qrev=dotf(flip_t,q[i0:i0+tile],1,0).astype(BF)
            dqr=dotf(rev,kd[start:start+width],1,0)
            dq=dotf(ds,k,1,0)+dotf(flip_t.astype(F32),dqr,1,0,hi)
            dq_ref[0,i0:i0+tile,cols]=dq.astype(BF)
            dkd_ref[start:start+width,cols]+=dotf(rev,qrev,0,0)
        dsf=ds_ref[...]
        dv_ref[0,:,cols]=dotf(pl_ref[...],dc,0,0).astype(BF)
        dkt_ref[...]=dotf(dsf,q,0,0)
        for j0 in range(0,total,TILE):
            width=rows+TILE; start=total-j0-TILE
            rev=dotf(flip_j,ds_ref[:,j0:j0+TILE],1,1).astype(BF)
            rev=jnp.concatenate([rev,jnp.zeros((TILE,TILE),BF)],axis=1)
            rev=pltpu.roll(rev,0,axis=1,stride=1,stride_axis=0)
            krev=dotf(flip_j,k[j0:j0+TILE],1,0).astype(BF)
            dkr=dotf(rev,pq[start:start+width],1,0)
            dk=dkt_ref[j0:j0+TILE,:]+dotf(flip_j.astype(F32),dkr,1,0,hi)
            dk_ref[0,j0:j0+TILE,cols]=dk.astype(BF)
            dpq_ref[start:start+width,cols]+=dotf(rev,krev,0,0)
        if between is not None:
            between(half)

def attend(q,k,v,kd,pq,sq,sk,scale):
    S,L,Wd=q.shape; T=k.shape[1]; W=kd.shape[0]; pairs=Wd//128
    row=lambda n:pl.BlockSpec((1,n,128),lambda s,h:(s,0,h))
    tab=pl.BlockSpec((W,128),lambda s,h:(0,h))
    return pl.pallas_call(functools.partial(attend_kernel,scale=scale),grid=(S,pairs),
      in_specs=[row(L),row(T),row(T),tab,tab,pl.BlockSpec((1,L,1),lambda s,h:(s,0,0)),pl.BlockSpec((1,1,T),lambda s,h:(s,0,0))],
      out_specs=[row(L),pl.BlockSpec((1,2,L,T),lambda s,h:(s,h,0,0))],
      out_shape=[jax.ShapeDtypeStruct((S,L,Wd),BF),jax.ShapeDtypeStruct((S,Wd//HD,L,T),F32)],
      scratch_shapes=[pltpu.VMEM((L,T),F32)],name="attend",
      cost_estimate=pl.CostEstimate(flops=int(16*S*L*T*Wd),bytes_accessed=int(S*L*T*Wd//HD*4),transcendentals=S*L*T*Wd//HD))(q,k,v,kd,pq,sq,sk)

def attend_back(q,k,v,kd,pq,p,dc,scale):
    S,L,Wd=q.shape; T=k.shape[1]; W=kd.shape[0]; pairs=Wd//128
    row=lambda n:pl.BlockSpec((1,n,128),lambda h,s:(s,0,h))
    tab=pl.BlockSpec((W,128),lambda h,s:(0,h))
    return pl.pallas_call(functools.partial(attend_back_kernel,scale=scale),grid=(pairs,S),
      in_specs=[row(L),row(T),row(T),tab,tab,pl.BlockSpec((1,2,L,T),lambda h,s:(s,h,0,0)),row(L)],
      out_specs=[row(L),row(T),row(T),tab,tab],
      out_shape=[jax.ShapeDtypeStruct((S,n,Wd),BF) for n in (L,T,T)]+[jax.ShapeDtypeStruct((W,Wd),F32)]*2,
      scratch_shapes=[pltpu.VMEM((L,T),BF),pltpu.VMEM((L,T),BF),pltpu.VMEM((T,HD),F32)],name="attend_back",
      cost_estimate=pl.CostEstimate(flops=int(32*S*L*T*Wd),bytes_accessed=int(S*L*T*Wd//HD*4),transcendentals=0))(q,k,v,kd,pq,p,dc)


BOTH = ("shard", "context")
eps_norm = 1e-06

MESH = pl.DeviceIdType.MESH
ROUNDS = 8


class Line:
    def __init__(self, n, chunk, send, from_left, from_right, total, sems):
        self.n, self.chunk, self.owner = n, chunk, n // 2 - 1
        self.send, self.from_left, self.from_right, self.total, self.sems = send, from_left, from_right, total, sems

    def at(self, half, k):
        p = lax.axis_index("tensor")
        rows = pl.ds(pl.multiple_of((2 * k + half) * self.chunk, self.chunk), self.chunk)
        q = p if half == 0 else self.n - 1 - p
        return q, p + 1 - 2 * half, p - 1 + 2 * half, rows

    def copy(self, half, k, kind, source, target, recv, device, rows):
        return pltpu.make_async_remote_copy(
            src_ref=source.at[rows, :], dst_ref=target.at[rows, :], send_sem=self.sems.at[kind, half, k],
            recv_sem=self.sems.at[recv, half, k], device_id={"tensor": device}, device_id_type=MESH)

    def inward_left(self, half, k):
        q, right, left, rows = self.at(half, k)
        return self.copy(half, k, 0, self.send, self.from_right, 2, left, rows)

    def inward_right(self, half, k):
        q, right, left, rows = self.at(half, k)
        return self.copy(half, k, 0, self.send, self.from_left, 1, right, rows)

    def outward_right(self, half, k):
        q, right, left, rows = self.at(half, k)
        return self.copy(half, k, 3, self.total, self.total, 5, right, rows)

    def outward_left(self, half, k):
        q, right, left, rows = self.at(half, k)
        return self.copy(half, k, 4, self.total, self.total, 5, left, rows)

    def edge(self, half, k):
        q = self.at(half, k)[0]

        @pl.when(q == self.n - 1)
        def _():
            self.inward_left(half, k).start()
        if self.owner > 0:
            @pl.when(q == 0)
            def _():
                self.inward_right(half, k).start()

    def mid(self, half, k):
        n, o = self.n, self.owner
        q, right, left, rows = self.at(half, k)
        if n - 1 - o > 1:
            @pl.when((q > o) & (q < n - 1))
            def _():
                self.inward_left(half, k).wait_recv()
                self.send[rows, :] = (self.send[rows, :].astype(F32) + self.from_right[rows, :].astype(F32)).astype(BF)
                self.inward_left(half, k).start()
        if o > 1:
            @pl.when((q < o) & (q > 0))
            def _():
                self.inward_right(half, k).wait_recv()
                self.send[rows, :] = (self.send[rows, :].astype(F32) + self.from_left[rows, :].astype(F32)).astype(BF)
                self.inward_right(half, k).start()

    def own(self, half, k):
        o = self.owner
        q, right, left, rows = self.at(half, k)

        @pl.when(q == o)
        def _():
            self.inward_left(half, k).wait_recv()
            total = self.send[rows, :].astype(F32) + self.from_right[rows, :].astype(F32)
            if o > 0:
                self.inward_right(half, k).wait_recv()
                total = total + self.from_left[rows, :].astype(F32)
            self.total[rows, :] = total.astype(BF)
            self.outward_right(half, k).start()
            if o > 0:
                self.outward_left(half, k).start()

    def forward(self, half, k):
        n, o = self.n, self.owner
        q = self.at(half, k)[0]

        @pl.when(q > o)
        def _():
            self.outward_right(half, k).wait_recv()

            @pl.when(q < n - 1)
            def _():
                self.outward_right(half, k).start()
        if o > 0:
            @pl.when(q < o)
            def _():
                self.outward_left(half, k).wait_recv()

                @pl.when(q > 0)
                def _():
                    self.outward_left(half, k).start()

    def drain(self, half, k):
        n, o = self.n, self.owner
        q = self.at(half, k)[0]

        @pl.when(q != o)
        def _():
            self.inward_left(half, k).wait_send()

        @pl.when((q >= o) & (q < n - 1))
        def _():
            self.outward_right(half, k).wait_send()
        if o > 0:
            @pl.when((q <= o) & (q > 0))
            def _():
                self.outward_left(half, k).wait_send()


def greet_line(n):
    p = lax.axis_index("tensor")
    barrier = pltpu.get_barrier_semaphore()

    @pl.when(p > 0)
    def _():
        pl.semaphore_signal(barrier, inc=1, device_id={"tensor": p - 1}, device_id_type=MESH)

    @pl.when(p < n - 1)
    def _():
        pl.semaphore_signal(barrier, inc=1, device_id={"tensor": p + 1}, device_id_type=MESH)

    inner = (p > 0) & (p < n - 1)

    @pl.when(inner)
    def _():
        pl.semaphore_wait(barrier, 2)

    @pl.when(jnp.logical_not(inner))
    def _():
        pl.semaphore_wait(barrier, 1)


def standardize(values):
    center = values - jnp.mean(values, axis=1, keepdims=True)
    rate = lax.rsqrt(jnp.mean(center * center, axis=1, keepdims=True) + eps_norm)
    return center * rate, rate


def norm_back(grad, unit, rate, gain):
    scaled = grad * gain
    return rate * (scaled - jnp.mean(scaled, axis=1, keepdims=True) - unit * jnp.mean(scaled * unit, axis=1, keepdims=True))


def middle_kernel(n, ctx, rows, wo_t, norms, cot_hbm, up_hbm, down_hbm, outputs, d_first, d_ctx, g_up, g_down, g_out, g_norm,
                  cot, up, down, low, act, d_ffn, d_hid, d_br, unit, slope, d_sec, rates, sums, load_sems, *line_refs):
    R, D = rows.shape
    chunk = R // (2 * ROUNDS)
    pair = 2 * chunk
    loads = [pltpu.make_async_copy(a, b, load_sems.at[i]) for i, (a, b) in
             enumerate([(up_hbm, up), (down_hbm, down), (cot_hbm, cot)])]
    for load in loads:
        load.start()
    lines = [Line(n, chunk, *line_refs[5 * i:5 * i + 5]) for i in range(3)]
    greet_line(n)
    sums[...] = jnp.zeros_like(sums)

    def add_sum(i, values):
        sums[8 * i:8 * i + 8, :] += jnp.sum(values.reshape(pair // 8, 8, D), axis=0)

    def pair_rows(k):
        return pl.ds(pl.multiple_of(k * pair, pair), pair)

    def open_first(k):
        r = pair_rows(k)
        lines[0].send[r, :] = dotf(ctx[r, :], wo_t[...], 1, 1).astype(BF)

    def first_to_second(k):
        r = pair_rows(k)
        u, rate = standardize(rows[r, :].astype(F32) + lines[0].total[r, :].astype(F32))
        unit[r, :] = u
        rates[r, :] = jnp.broadcast_to(rate, (pair, 128))
        nl = (u * norms[0:1, :] + norms[1:2, :]).astype(BF)
        low[r, :] = nl
        hidden = dotf(nl, up[...], 1, 0)
        half_cdf = 0.5 * (1.0 + lax.erf(hidden * 0.7071067811865476))
        slope[r, :] = half_cdf + hidden * (jnp.exp(-0.5 * hidden * hidden) * 0.3989422804014327)
        a = (hidden * half_cdf).astype(BF)
        act[r, :] = a
        lines[1].send[r, :] = dotf(a, down[...], 1, 1).astype(BF)

    def second_to_third(k):
        r = pair_rows(k)
        u, rate = standardize(unit[r, :] * norms[0:1, :] + norms[1:2, :] + lines[1].total[r, :].astype(F32))
        outputs[r, :] = (u * norms[2:3, :] + norms[3:4, :]).astype(BF)
        g = cot[r, :].astype(F32)
        add_sum(2, g * u)
        add_sum(3, g)
        ds = norm_back(g, u, rate, norms[2:3, :])
        d_sec[r, :] = ds
        dl = ds.astype(BF)
        d_ffn[r, :] = dl
        dh = (dotf(dl, down[...], 1, 0) * slope[r, :]).astype(BF)
        d_hid[r, :] = dh
        lines[2].send[r, :] = dotf(dh, up[...], 1, 1).astype(BF)

    def close_third(k):
        r = pair_rows(k)
        g = d_sec[r, :] + lines[2].total[r, :].astype(F32)
        u = unit[r, :]
        add_sum(0, g * u)
        add_sum(1, g)
        d1 = norm_back(g, u, rates[r, 0:1], norms[0:1, :])
        d_first[r, :] = d1
        db = d1.astype(BF)
        d_br[r, :] = db
        d_ctx[r, :] = dotf(db, wo_t[...], 1, 0).astype(BF)

    def weight_grad(out, left, right):
        width = min(256, D)

        def tile(i, _):
            c = pl.ds(pl.multiple_of(i * width, width), width)
            out[c, :] = dotf(left[:, c], right[...], 0, 0).astype(BF)
            return 0
        lax.fori_loop(0, D // width, tile, 0)

    def when_valid(t, lag, body):
        @pl.when((t >= lag) & (t < lag + ROUNDS))
        def _():
            body(t - lag)

    def both(stage):
        def run(k):
            stage(0, k)
            stage(1, k)
        return run

    def start(line, body):
        def run(k):
            body(k)
            line.edge(0, k)
            line.edge(1, k)
        return run

    def step(t, _):
        for i in (2, 1, 0):
            for lag, stage in ((8, lines[i].forward), (6, lines[i].own), (4, lines[i].mid)):
                when_valid(t, 8 * i + lag, both(stage))
        when_valid(t, 24, close_third)
        when_valid(t, 16, start(lines[2], second_to_third))
        when_valid(t, 8, start(lines[1], first_to_second))
        when_valid(t, 0, start(lines[0], open_first))

        @pl.when(t == 7)
        def _():
            for load in loads:
                load.wait()

        @pl.when(t == 16 + ROUNDS)
        def _():
            weight_grad(g_down, d_ffn, act)

        @pl.when(t == 17 + ROUNDS)
        def _():
            weight_grad(g_up, low, d_hid)
        return 0

    lax.fori_loop(0, ROUNDS + 24, step, 0)
    weight_grad(g_out, d_br, ctx)
    for i in range(4):
        g_norm[i:i + 1, :] = jnp.sum(sums[8 * i:8 * i + 8, :], axis=0, keepdims=True)
    g_norm[4:8, :] = jnp.zeros((4, D), F32)

    def finish(k, _):
        for line in lines:
            line.drain(0, k)
            line.drain(1, k)
        return 0
    lax.fori_loop(0, ROUNDS, finish, 0)


def middle(n, ctx, rows, wo_t, norms, cot, up, down):
    R, D = rows.shape
    Wd, F = wo_t.shape[1], up.shape[1]
    vmem, hbm = pl.BlockSpec(memory_space=pltpu.VMEM), pl.BlockSpec(memory_space=pl.ANY)
    line = [pltpu.VMEM((R, D), BF)] * 4 + [pltpu.SemaphoreType.DMA((6, 2, ROUNDS))]
    shape = jax.ShapeDtypeStruct
    return pl.pallas_call(
        partial(middle_kernel, n),
        in_specs=[vmem] * 4 + [hbm] * 3,
        out_specs=[vmem] * 7,
        out_shape=[shape((R, D), BF), shape((R, D), F32), shape((R, Wd), BF), shape((D, F), BF), shape((D, F), BF),
                   shape((D, Wd), BF), shape((8, D), F32)],
        scratch_shapes=[pltpu.VMEM((R, D), BF), pltpu.VMEM((D, F), BF), pltpu.VMEM((D, F), BF), pltpu.VMEM((R, D), BF),
                        pltpu.VMEM((R, F), BF), pltpu.VMEM((R, D), BF), pltpu.VMEM((R, F), BF), pltpu.VMEM((R, D), BF),
                        pltpu.VMEM((R, D), F32), pltpu.VMEM((R, F), F32), pltpu.VMEM((R, D), F32), pltpu.VMEM((R, 128), F32),
                        pltpu.VMEM((32, D), F32), pltpu.SemaphoreType.DMA((3,))] + line * 3,
        compiler_params=pltpu.CompilerParams(collective_id=1, has_side_effects=True),
        name="middle",
        cost_estimate=pl.CostEstimate(flops=12 * R * D * F, bytes_accessed=16 * R * D, transcendentals=2 * R * F),
    )(ctx, rows, wo_t, norms, cot, up, down)


def plane_peers():
    s, c = lax.axis_index("shard"), lax.axis_index("context")
    near = [s, s + 1 - 2 * (s % 2), (s + 2) % 4, 3 - s]
    return near, c


def greet_plane():
    near, c = plane_peers()
    barrier = pltpu.get_barrier_semaphore()
    pl.semaphore_signal(barrier, inc=1, device_id={"context": 1 - c}, device_id_type=MESH)
    for j in (1, 2):
        pl.semaphore_signal(barrier, inc=1, device_id={"shard": near[j]}, device_id_type=MESH)
    pl.semaphore_wait(barrier, 3)


class Scatter:
    def __init__(self, mats, partner_in, acc, corner_in, came, sems, loads=None):
        self.mats, self.partner_in, self.acc, self.corner_in, self.came = mats, partner_in, acc, corner_in, came
        self.sems, self.loads = sems, loads
        self.own = corner_in.shape[1]

    def block(self, j):
        return pl.ds(j * self.own, self.own)

    def source(self, side, j, other):
        near, c = plane_peers()
        core = 1 - c if other else c
        return self.mats[side].at[pl.ds(pl.multiple_of((2 * near[j] + core) * self.own, self.own), self.own), :]

    def to_partner(self, side, j):
        c = lax.axis_index("context")
        return pltpu.make_async_remote_copy(
            src_ref=self.source(side, j, True), dst_ref=self.partner_in.at[side, self.block(j), :],
            send_sem=self.sems.at[0, side, j], recv_sem=self.sems.at[1, side, j], device_id={"context": 1 - c}, device_id_type=MESH)

    def load(self, side, j):
        return pltpu.make_async_copy(self.source(side, j, False), self.acc.at[side, self.block(j), :], self.loads.at[side, j])

    def hop(self, side, j, axis, target, kind):
        near, _ = plane_peers()
        return pltpu.make_async_remote_copy(
            src_ref=self.acc.at[side, self.block(j), :], dst_ref=target, send_sem=self.sems.at[2, side, kind],
            recv_sem=self.sems.at[3, side, kind], device_id={"shard": near[axis]}, device_id_type=MESH)

    def corner(self, side):
        return self.hop(side, 3, 1 + side, self.corner_in.at[side], 0)

    def early(self, side):
        return self.hop(side, 1 + side, 1 + side, self.came.at[side, 0], 1)

    def late(self, side):
        return self.hop(side, 2 - side, 2 - side, self.came.at[side, 1], 2)

    def begin(self, side):
        for j in (3, 1, 2, 0):
            self.to_partner(side, j).start()
            if self.loads is not None:
                self.load(side, j).start()

    def add_partner(self, side, j):
        self.to_partner(side, j).wait_recv()
        if self.loads is not None:
            self.load(side, j).wait()
            mine = self.acc[side, self.block(j), :]
        else:
            mine = self.source(side, j, False)[...]
        self.acc[side, self.block(j), :] = (mine.astype(F32) + self.partner_in[side, self.block(j), :].astype(F32)).astype(BF)

    def spread(self, side):
        self.add_partner(side, 3)
        self.corner(side).start()
        self.add_partner(side, 1 + side)
        self.early(side).start()
        self.add_partner(side, 2 - side)
        self.add_partner(side, 0)

    def turn(self, side):
        self.corner(side).wait_recv()
        b = self.block(2 - side)
        self.acc[side, b, :] = (self.acc[side, b, :].astype(F32) + self.corner_in[side].astype(F32)).astype(BF)
        self.late(side).start()

    def result(self, side):
        self.early(side).wait_recv()
        self.late(side).wait_recv()
        return (self.acc[side, self.block(0), :].astype(F32) + self.came[side, 0].astype(F32) + self.came[side, 1].astype(F32))

    def drain(self, side):
        for j in range(4):
            self.to_partner(side, j).wait_send()
        self.corner(side).wait_send()
        self.early(side).wait_send()
        self.late(side).wait_send()


def scatter_scratch(own, width, load):
    shapes = [pltpu.VMEM((2, 4 * own, width), BF), pltpu.VMEM((2, 4 * own, width), BF), pltpu.VMEM((2, own, width), BF),
              pltpu.VMEM((2, 2, own, width), BF), pltpu.SemaphoreType.DMA((4, 2, 4))]
    return shapes + ([pltpu.SemaphoreType.DMA((2, 4))] if load else [])


def attend_back_scatter_kernel(*refs, scale):
    ins, (g_up, g_down), outs, (o_up, o_down), scratch, shared = refs[:7], refs[7:9], refs[9:14], refs[14:16], refs[16:19], refs[19:]
    job = Scatter((g_up, g_down), *shared)
    step, last = pl.program_id(0), pl.num_programs(0) - 1

    @pl.when(step == 0)
    def _():
        greet_plane()
        job.begin(0)
        job.begin(1)

    def between(half):
        if half == 0:
            @pl.when(step == 0)
            def _():
                job.spread(0)
                job.spread(1)
        else:
            @pl.when(step == 0)
            def _():
                job.turn(0)
                job.turn(1)

    attend_back_kernel(*ins, *outs, *scratch, scale=scale, between=between)

    @pl.when(step == last)
    def _():
        o_up[...] = job.result(0)
        o_down[...] = job.result(1).T
        job.drain(0)
        job.drain(1)


def attend_back_scatter(q, k, v, kd, pq, p, dc, g_up, g_down, scale):
    S, L, Wd = q.shape
    T = k.shape[1]
    W = kd.shape[0]
    D, F = g_up.shape
    own, pairs = D // 8, Wd // 128
    row = lambda n: pl.BlockSpec((1, n, 128), lambda h, s: (s, 0, h))
    tab = pl.BlockSpec((W, 128), lambda h, s: (0, h))
    hbm = pl.BlockSpec(memory_space=pl.ANY)
    fixed = lambda *shape: pl.BlockSpec(shape, lambda h, s: (0, 0))
    return pl.pallas_call(
        partial(attend_back_scatter_kernel, scale=scale), grid=(pairs, S),
        in_specs=[row(L), row(T), row(T), tab, tab, pl.BlockSpec((1, 2, L, T), lambda h, s: (s, h, 0, 0)), row(L), hbm, hbm],
        out_specs=[row(L), row(T), row(T), tab, tab, fixed(own, F), fixed(F, own)],
        out_shape=[jax.ShapeDtypeStruct((S, n, Wd), BF) for n in (L, T, T)] + [jax.ShapeDtypeStruct((W, Wd), F32)] * 2
        + [jax.ShapeDtypeStruct((own, F), F32), jax.ShapeDtypeStruct((F, own), F32)],
        scratch_shapes=[pltpu.VMEM((L, T), BF), pltpu.VMEM((L, T), BF), pltpu.VMEM((T, HD), F32)] + scatter_scratch(own, F, True),
        compiler_params=pltpu.CompilerParams(collective_id=3, has_side_effects=True),
        name="attend_back",
        cost_estimate=pl.CostEstimate(flops=int(32 * S * L * T * Wd), bytes_accessed=int(S * L * T * Wd // HD * 4), transcendentals=0),
    )(q, k, v, kd, pq, p, dc, g_up, g_down)


def tail_kernel(n, dq, dk, dv, wqkv, rows, d_first, pos_t, to_row, from_row, dkd, dpq, g_out, g_norm,
                grad_in, o_q, o_k, o_v, o_out, o_pos, o_norm,
                k_in, v_in, dqkv, d_pos, g_left, g_right, norm_in, swap_sems, norm_sems, *refs):
    L, Wd = dq.shape
    D, B = pos_t.shape
    W = to_row.shape[1]
    own = D // 8
    chunk = L // (2 * ROUNDS)
    pair = 2 * chunk
    line = Line(n, chunk, *refs[:5])
    small = Line(n, own // 2, *refs[5:10])
    job = Scatter((g_left, g_right), *refs[10:])
    near, c = plane_peers()
    p = lax.axis_index("tensor")
    barrier = pltpu.get_barrier_semaphore()
    for j in range(4):
        for core in (c, 1 - c):
            if j > 0 or core is not c:
                pl.semaphore_signal(barrier, inc=1, device_id={"shard": near[j], "context": core}, device_id_type=MESH)

    @pl.when(p > 0)
    def _():
        pl.semaphore_signal(barrier, inc=1, device_id={"tensor": p - 1}, device_id_type=MESH)

    @pl.when(p < n - 1)
    def _():
        pl.semaphore_signal(barrier, inc=1, device_id={"tensor": p + 1}, device_id_type=MESH)
    inner = (p > 0) & (p < n - 1)

    @pl.when(inner)
    def _():
        pl.semaphore_wait(barrier, 9)

    @pl.when(jnp.logical_not(inner))
    def _():
        pl.semaphore_wait(barrier, 8)

    def swap(i, source, target):
        part = pl.ds(pl.multiple_of((1 - c) * L, L), L)
        return pltpu.make_async_remote_copy(src_ref=source.at[part, :], dst_ref=target, send_sem=swap_sems.at[0, i],
                                            recv_sem=swap_sems.at[1, i], device_id={"context": 1 - c}, device_id_type=MESH)
    swaps = [swap(0, dk, k_in), swap(1, dv, v_in)]
    for s in swaps:
        s.start()
    pieces = []
    for j in range(4):
        for other in range(2):
            core = c if other == 0 else 1 - c
            if j == 0 and other == 0:
                continue
            i = 2 * j + other
            lanes = pl.ds(pl.multiple_of((2 * near[j] + core) * own, own), own)
            pieces.append(pltpu.make_async_remote_copy(
                src_ref=g_norm.at[:, lanes], dst_ref=norm_in.at[i], send_sem=norm_sems.at[0, i], recv_sem=norm_sems.at[1, i],
                device_id={"shard": near[j], "context": core}, device_id_type=MESH))
    for piece in pieces:
        piece.start()

    ids = lax.broadcasted_iota(jnp.int32, (B, W), 0)
    d_pos[:, :Wd] = dotf((ids == from_row[...]).astype(F32).astype(BF), dpq[...].astype(BF), 1, 0).astype(BF)
    d_pos[:, Wd:] = dotf((ids == to_row[...]).astype(F32).astype(BF), dkd[...].astype(BF), 1, 0).astype(BF)
    g_right[:, :Wd] = g_out[...]
    width = 256

    def right_tile(i, _):
        r = pl.ds(pl.multiple_of(i * width, width), width)
        g_right[r, Wd:] = dotf(wqkv[r, :2 * Wd], d_pos[...], 1, 1).astype(BF)
        return 0
    lax.fori_loop(0, D // width, right_tile, 0)
    job.begin(1)
    here = pl.ds(pl.multiple_of(c * L, L), L)
    dqkv[:, :Wd] = dq[...]
    for s, mine, got, at in ((swaps[0], dk, k_in, Wd), (swaps[1], dv, v_in, 2 * Wd)):
        s.wait_recv()
        dqkv[:, at:at + Wd] = (mine[here, :].astype(F32) + got[...].astype(F32)).astype(BF)

    def pair_rows(k):
        return pl.ds(pl.multiple_of(k * pair, pair), pair)

    def produce(k, _):
        r = pair_rows(k)
        line.send[r, :] = dotf(dqkv[r, :], wqkv[...], 1, 1).astype(BF)
        line.edge(0, k)
        line.edge(1, k)
        return 0
    lax.fori_loop(0, ROUNDS, produce, 0)

    def left_tile(i, _):
        r = pl.ds(pl.multiple_of(i * width, width), width)
        g = dotf(rows[:, r], dqkv[...], 0, 0)
        g_left[r, :2 * Wd] = (g[:, :2 * Wd] + dotf(pos_t[r, :], d_pos[...], 1, 0)).astype(BF)
        g_left[r, 2 * Wd:] = g[:, 2 * Wd:].astype(BF)
        return 0
    lax.fori_loop(0, D // width, left_tile, 0)
    job.begin(0)
    job.spread(1)

    def step(t, _):
        for lag, stage in ((4, line.forward), (2, line.own), (0, line.mid)):
            @pl.when((t >= lag) & (t < lag + ROUNDS))
            def _():
                stage(0, t - lag)
                stage(1, t - lag)

        @pl.when((t >= 4) & (t < 4 + ROUNDS))
        def _():
            r = pair_rows(t - 4)
            grad_in[r, :] = (d_first[r, :] + line.total[r, :].astype(F32)).astype(BF)

        @pl.when(t == 0)
        def _():
            job.spread(0)

        @pl.when(t == 2)
        def _():
            job.turn(1)
            job.turn(0)

        @pl.when(t == 6)
        def _():
            right = job.result(1)
            o_out[...] = right[:, :Wd].T
            small.send[...] = right[:, Wd:].astype(BF)
            small.edge(0, 0)
            small.edge(1, 0)

        @pl.when(t == 7)
        def _():
            left = job.result(0)
            o_q[...] = left[:, :Wd]
            o_k[...] = left[:, Wd:2 * Wd]
            o_v[...] = left[:, 2 * Wd:]

        for at, stage in ((8, small.mid), (9, small.own), (11, small.forward)):
            @pl.when(t == at)
            def _():
                stage(0, 0)
                stage(1, 0)
        return 0
    lax.fori_loop(0, ROUNDS + 4, step, 0)
    o_pos[...] = small.total[...].astype(F32).T
    lanes = pl.ds(pl.multiple_of((2 * near[0] + c) * own, own), own)
    total = g_norm[:, lanes]
    for piece in pieces:
        piece.wait_recv()
    for i in range(1, 8):
        total = total + norm_in[i]
    o_norm[...] = total

    def finish(k, _):
        line.drain(0, k)
        line.drain(1, k)
        return 0
    lax.fori_loop(0, ROUNDS, finish, 0)
    small.drain(0, 0)
    small.drain(1, 0)
    job.drain(0)
    job.drain(1)
    for copy in swaps + pieces:
        copy.wait_send()


def tail(n, dq, dk, dv, wqkv, rows, d_first, pos_t, to_row, from_row, dkd, dpq, g_out, g_norm):
    L, Wd = dq.shape
    D, B = pos_t.shape
    own = D // 8
    vmem = pl.BlockSpec(memory_space=pltpu.VMEM)
    shape = jax.ShapeDtypeStruct
    line = [pltpu.VMEM((L, D), BF)] * 4 + [pltpu.SemaphoreType.DMA((6, 2, ROUNDS))]
    small = [pltpu.VMEM((own, B), BF)] * 4 + [pltpu.SemaphoreType.DMA((6, 2, 1))]
    return pl.pallas_call(
        partial(tail_kernel, n),
        in_specs=[vmem] * 13, out_specs=[vmem] * 7,
        out_shape=[shape((L, D), BF)] + [shape((own, Wd), F32)] * 3 + [shape((Wd, own), F32), shape((B, own), F32), shape((8, own), F32)],
        scratch_shapes=[pltpu.VMEM((L, Wd), BF), pltpu.VMEM((L, Wd), BF), pltpu.VMEM((L, 3 * Wd), BF), pltpu.VMEM((B, 2 * Wd), BF),
                        pltpu.VMEM((D, 3 * Wd), BF), pltpu.VMEM((D, Wd + B), BF), pltpu.VMEM((8, 8, own), F32),
                        pltpu.SemaphoreType.DMA((2, 2)), pltpu.SemaphoreType.DMA((2, 8))] + line + small
        + scatter_scratch(own, 3 * Wd, False),
        compiler_params=pltpu.CompilerParams(collective_id=4, has_side_effects=True),
        name="tail",
        cost_estimate=pl.CostEstimate(flops=8 * L * D * 3 * Wd, bytes_accessed=16 * L * D, transcendentals=0),
    )(dq, dk, dv, wqkv, rows, d_first, pos_t, to_row, from_row, dkd, dpq, g_out, g_norm)


def split_columns(packed, widths):
    at, out = 0, []
    for width in widths:
        out.append(packed[:, at:at + width])
        at += width
    return out


def local(inputs, cotangent, segments, buckets, w_query, w_key, w_value, w_output, w_up, w_down,
          positions, gain_attn, bias_attn, gain_ffn, bias_ffn):
    S, L, D = inputs.shape
    T = segments.shape[1]
    Wd = w_query.shape[1]
    F = w_up.shape[1]
    B = positions.shape[0]
    scale = 1.0 / math.sqrt(3 * HD)
    first = lax.axis_index("context") * L
    W = T + L
    own = w_query.shape[0]
    norms = jnp.stack([gain_attn, bias_attn, gain_ffn, bias_ffn], axis=1)
    norms = jnp.pad(norms, ((0, 0), (0, 124)))
    pack = jnp.concatenate([w_query, w_key, w_value, w_output.T, positions.T, norms], axis=1)
    pack = lax.all_gather(pack, BOTH, axis=0, tiled=True)
    wq, wk, wv, wo_t, pos_t, norms = split_columns(pack, (Wd, Wd, Wd, Wd, B, 128))
    ffn = lax.all_gather(jnp.concatenate([w_up, w_down.T], axis=1), BOTH, axis=0, tiled=True)
    up, down_t = split_columns(ffn, (F, F))
    norms = jnp.pad(norms[:, :4].astype(F32).T, ((0, 4), (0, 0)))
    rows = inputs.reshape(S * L, D)
    wqkv = pack[:, :3 * Wd]
    qkv = dotf(rows, wqkv, 1, 0).astype(BF)
    q, k, v = [x.reshape(S, L, Wd) for x in split_columns(qkv, (Wd, Wd, Wd))]
    k, v = split_last(lax.all_gather(jnp.concatenate([k, v], axis=2), "context", axis=1, tiled=True), Wd)
    pos_qk = dotf(pos_t, jnp.concatenate([wq, wk], axis=1), 0, 0).astype(BF)
    flipped = jnp.concatenate([buckets[::-1], buckets[:1]])
    to = lax.dynamic_slice_in_dim(flipped, T - L - first, W, 0)
    fro = lax.dynamic_slice_in_dim(flipped, first, W, 0)
    ids = jnp.arange(B, dtype=jnp.int32)
    pick_to = (to[:, None] == ids[None]).astype(BF)
    pick_from = (fro[:, None] == ids[None]).astype(BF)
    kd = dotf(pick_to, pos_qk[:, Wd:], 1, 0).astype(BF)
    pq = dotf(pick_from, pos_qk[:, :Wd], 1, 0).astype(BF)
    seg_here = lax.dynamic_slice_in_dim(segments, first, L, 1)[:, :, None]
    ctx, probs = attend(q, k, v, kd, pq, seg_here, segments[:, None, :], scale)
    ctx_rows = ctx.reshape(S * L, Wd)
    outputs, d_first, d_ctx, g_up, g_down_t, g_out_t, g_norm = middle(
        lax.axis_size("tensor"), ctx_rows, rows, wo_t, norms, cotangent.reshape(S * L, D), up, down_t)
    outputs = outputs.reshape(inputs.shape)
    f = lambda x: x.astype(F32)
    if (lax.axis_size("shard"), lax.axis_size("context"), S, own * 8, 3 * Wd) == (4, 2, 1, D, Wd + B):
        dq, dk, dv, dkd, dpq, g_up, g_down = attend_back_scatter(q, k, v, kd, pq, probs, d_ctx.reshape(S, L, Wd), g_up, g_down_t, scale)
        grad_inputs, g_q, g_k, g_v, g_o, g_p, g_n = tail(
            lax.axis_size("tensor"), dq[0], dk[0], dv[0], wqkv, rows, d_first, pos_t, to[None], fro[None], dkd, dpq, g_out_t, g_norm)
        return (outputs, grad_inputs.reshape(inputs.shape), g_q, g_k, g_v, g_o, g_up, g_down, g_p, g_n[0], g_n[1], g_n[2], g_n[3])
    scatter = partial(lax.psum_scatter, axis_name=BOTH, scatter_dimension=0, tiled=True)
    g_ffn = scatter(jnp.concatenate([g_up, g_down_t], axis=1))
    dq, dk, dv, dkd, dpq = attend_back(q, k, v, kd, pq, probs, d_ctx.reshape(S, L, Wd), scale)
    dkv = lax.psum_scatter(jnp.concatenate([dk, dv], axis=2), "context", scatter_dimension=1, tiled=True)
    dqkv = jnp.concatenate([dq, dkv], axis=2).reshape(S * L, 3 * Wd)
    weights = jnp.concatenate([wq, wk, wv], axis=1)
    d_in = lax.psum(dotf(dqkv, weights, 1, 1).astype(BF), "tensor").astype(F32)
    grad_inputs = (d_first + d_in).astype(BF).reshape(inputs.shape)
    d_pos_key = dotf(pick_to, dkd.astype(BF), 0, 0)
    d_pos_query = dotf(pick_from, dpq.astype(BF), 0, 0)
    d_pos = jnp.concatenate([d_pos_query, d_pos_key], axis=1).astype(BF)
    g_qkv = dotf(rows, dqkv, 0, 0)
    g_pos_t = dotf(jnp.concatenate([wq, wk], axis=1), d_pos, 1, 1)
    g_qk = g_qkv[:, :2 * Wd] + dotf(pos_t, d_pos, 1, 0)
    g_norm = jnp.pad(g_norm.T, ((0, 0), (0, 120)))
    pack = jnp.concatenate([x.astype(BF) for x in (g_qk, g_qkv[:, 2 * Wd:], g_out_t, g_pos_t, g_norm)], axis=1)
    g_q, g_k, g_v, g_o, g_p, g_n = split_columns(scatter(pack), (Wd, Wd, Wd, Wd, B, 128))
    g_p = lax.psum(g_p, "tensor")
    return (outputs, grad_inputs, f(g_q), f(g_k), f(g_v), f(g_o).T, f(g_ffn[:, :F]), f(g_ffn[:, F:]).T, f(g_p).T,
            f(g_n[:, 0]), f(g_n[:, 1]), f(g_n[:, 2]), f(g_n[:, 3]))


def split_last(packed, width):
    return packed[..., :width], packed[..., width:]


def solution(mesh):
    P = jax.sharding.PartitionSpec
    act, row, col, vec = P("shard", "context", None), P(BOTH, "tensor"), P("tensor", BOTH), P(BOTH)
    return jax.shard_map(local, mesh=mesh,
        in_specs=(act, act, P("shard", None), P(), row, row, row, col, row, col, P(None, BOTH), vec, vec, vec, vec),
        out_specs=(act, act, row, row, row, col, row, col, P(None, BOTH), vec, vec, vec, vec),
        check_vma=False)
```

profile of v0, /device:TPU:0, one launch (start us, length us, event | category | flops | bytes accessed | tf_op | source)
XLA Modules:
  0.0 307.8 jit_solution(15031478959216659124)
XLA Ops:
  7.2 0.7 pad_maximum_fusion.2
  7.9 0.1 copy.56
  8.1 0.9 copy.54
  9.0 1.0 copy.55
  10.0 0.8 constant_dynamic-update-slice_fusion.2
  10.9 0.8 constant_dynamic-update-slice_fusion.1
  11.7 0.8 constant_dynamic-update-slice_fusion
  12.6 0.7 copy-done.3
  13.4 0.0 all-gather.6.cloned.1.call-start
  13.5 36.1 %all-gather.4.cloned.1.call-done = bf16[1024,1664]{1,0:T(8,128)(2,1)} async-done(((bf16[128,1664]{1,0:T(8,128)(2,1)}), bf16[1024,1664]{1,0:T(8,128)(2,1)}) %all-gather.4.cloned.1.call-update) | async-done | bytes 3407888 | tf_op jit(solution)/shard_map/all_gather | solution.py:778
  49.6 2.7 fusion.6
  52.3 0.8 slice_bitcast_fusion.2
  53.0 0.8 pad_maximum_fusion
  53.9 0.0 all-gather.8.cloned.1.call-start
  53.9 2.1 copy.59
  56.1 1.9 pad_maximum_fusion.1
  58.0 0.5 slice.65
  58.5 0.1 reverse
  58.6 0.1 slice.106
  58.7 0.7 dynamic-slice_add_fusion
  59.4 0.6 broadcast_in_dim.19.from_row
  60.0 0.6 broadcast_in_dim.18.to_row
  60.6 0.9 copy.58.sq_ref
  61.5 0.8 pad_convert_fusion
  62.3 1.8 copy.60.norms
  64.2 0.8 slice.86.wo_t
  65.0 1.0 slice.83.pos_t
  66.0 1.2 slice.77.wqkv
  67.3 0.7 convolution_convert_fusion.1
  68.0 1.6 fusion.2.pq_ref.refs_4_
  69.6 1.6 fusion.3.kd_ref.refs_3_
  71.2 2.2 fusion.14
  73.4 21.7 %attend.1 = (bf16[1,512,256]{2,1,0:T(8,128)(2,1)}, f32[1,4,512,1024]{3,2,1,0:T(8,128)}) custom-call(bf16[1,512,256]{2,1,0:T(8,128)(2,1)} %get-tuple-element.65.q_ref.refs_0_, bf16[1,1024,256]{2,1,0:T(8,128)(2,1)} %get-tuple-element.62.k_ref.refs_1_, bf16[1,1024,256]{2,1,0:T(8,128)(2,1)} %get-tuple-element.61.v_ref.refs_2_, ...), custom_call_target="tpu_custom_call" | custom-call | flops 2147483648 | bytes 8388608 | tf_op jit(solution)/shard_map/attend/pallas_call | solution.py:93
  95.1 7.6 %all-gather.8.cloned.1.call-done = bf16[1024,2048]{1,0:T(8,128)(2,1)} async-done(((bf16[128,2048]{1,0:T(8,128)(2,1)}), bf16[1024,2048]{1,0:T(8,128)(2,1)}) %all-gather.8.cloned.1.call-update) | async-done | bytes 4194320 | tf_op jit(solution)/shard_map/all_gather | solution.py:780
  102.8 4.6 %fusion.13 = (bf16[1024,1024]{1,0:T(8,128)(2,1)}, bf16[1024,1024]{1,0:T(8,128)(2,1)}) fusion(bf16[1024,2048]{1,0:T(8,128)(2,1)} %all-gather.8.cloned.1.call-done), kind=kLoop, calls=%fused_computation.38 | loop fusion | bytes 8388608 | tf_op jit(solution)/shard_map/slice | solution.py:759
  107.4 93.2 %middle.1 = (bf16[512,1024]{1,0:T(8,128)(2,1)}, f32[512,1024]{1,0:T(8,128)}, bf16[512,256]{1,0:T(8,128)(2,1)}, bf16[1024,1024]{1,0:T(8,128)(2,1)}, bf16[1024,102...) custom-call(bf16[512,256]{1,0:T(8,128)(2,1)} %bitcast.58, bf16[512,1024]{1,0:T(8,128)(2,1)} %bitcast.52, ...), custom_call_target="tpu_custom_call" | custom-call | flops 6442450944 | bytes 8388608 | tf_op jit(solution)/shard_map/middle/pallas_call | solution.py:399
  200.6 41.4 %attend_back.1 = (bf16[1,512,256]{2,1,0:T(8,128)(2,1)}, bf16[1,1024,256]{2,1,0:T(8,128)(2,1)}, bf16[1,1024,256]{2,1,0:T(8,128)(2,1)}, f32[1536,256]{1,0:T(8,128)...) custom-call(bf16[1,512,256]{2,1,0:T(8,128)(2,1)} %get-tuple-element.65.q_ref.refs_0_, ...), custom_call_target="tpu_custom_call" | custom-call | flops 4294967296 | bytes 8388608 | tf_op jit(solution)/shard_map/attend_back/pallas_call | solution.py:559
  242.1 50.9 %tail.1 = (bf16[512,1024]{1,0:T(8,128)(2,1)}, f32[128,256]{1,0:T(8,128)}, f32[128,256]{1,0:T(8,128)}, f32[128,256]{1,0:T(8,128)}, f32[256,128]{1,0:T(8,128)}, /*index=5*/f32[512,128]{1,0:T(8,128)}, f32[8,128]{1,0:T(8,128)}) custom-call(bf16[512,256]{1,0:T(8,128)(2,1)} %bitcast.56, bf16[1024,256]{1,0:T(8,128)(2,1)} %bitcast.54, bf16[1024,256]{1,0:T(8,128)(2,1)} %bitcast.55, ...), custom_call_target="tpu_custom_call" | custom-call | flops 3221225472 | bytes 8388608 | tf_op jit(solution)/shard_map/tail/pallas_call | solution.py:742
  293.0 1.4 slice_bitcast_fusion.4
  294.4 1.0 copy.76
  295.4 1.0 copy.77
  296.4 0.7 copy.78
  297.0 0.7 copy.79
  297.7 0.7 copy.80
  298.3 0.7 copy.81
  299.0 0.8 copy.82
  299.8 0.8 copy.83
  300.6 0.7 copy.84
  (35 shorter events, 0.2 us)
Async XLA Ops:
  7.2 42.4 %all-gather.4.cloned.1.call-start = ((), (), s32[]{:S(2)}) async-start(), calls=%async_computation | async-start | bytes 3833856 | tf_op jit(solution)/shard_map/all_gather | solution.py:778
  12.6 0.8 copy-start.3
  13.4 57.8 %all-gather.6.cloned.1.call-start = ((), (), s32[]{:S(2)}) async-start(), calls=%async_computation.1 | async-start | bytes 1572864 | tf_op jit(solution)/shard_map/all_gather | solution.py:787
  53.0 4.9 %copy-start.11 = (s32[2047]{0:T(1024)S(1)}, s32[2047]{0:T(1024)}, u32[]{:S(2)}) copy-start(s32[2047]{0:T(1024)} %param.18) | copy-start | bytes 24568
  53.0 7.6 %copy-start.12 = (s32[1,1024]{1,0:T(1,128)S(1)}, s32[1,1024]{1,0:T(1,128)}, u32[]{:S(2)}) copy-start(s32[1,1024]{1,0:T(1,128)} %param.17) | copy-start | bytes 12292
  53.0 8.4 %copy-start = (bf16[1024,1664]{1,0:T(8,128)(2,1)S(1)}, bf16[1024,1664]{1,0:T(8,128)(2,1)}, u32[]{:S(2)}) copy-start(bf16[1024,1664]{1,0:T(8,128)(2,1)} %all-gather.4.cloned.1.call-done) | copy-start | bytes 10223620
  53.9 48.9 %all-gather.8.cloned.1.call-start = ((), (), s32[]{:S(2)}) async-start(), calls=%async_computation.2 | async-start | bytes 4718592 | tf_op jit(solution)/shard_map/all_gather | solution.py:780
  242.1 52.3 %copy-start.1 = (bf16[512,1024]{1,0:T(8,128)(2,1)S(1)}, bf16[512,1024]{1,0:T(8,128)(2,1)}, u32[]{:S(2)}) copy-start(bf16[512,1024]{1,0:T(8,128)(2,1)} %get-tuple-element.37) | copy-start | bytes 3145732
  293.0 2.4 copy-start.2
  294.4 2.0 copy-start.10
  294.4 2.6 copy-start.9
  294.4 3.3 %copy-start.8 = (f32[128,256]{1,0:T(8,128)S(1)}, f32[128,256]{1,0:T(8,128)}, u32[]{:S(2)}) copy-start(f32[128,256]{1,0:T(8,128)} %get-tuple-element.89) | copy-start | bytes 393220
  294.4 3.9 %copy-start.7 = (f32[256,128]{1,0:T(8,128)S(1)}, f32[256,128]{1,0:T(8,128)}, u32[]{:S(2)}) copy-start(f32[256,128]{1,0:T(8,128)} %get-tuple-element.90) | copy-start | bytes 393220
  295.4 3.6 %copy-start.5 = (f32[128,1024]{1,0:T(8,128)S(1)}, f32[128,1024]{1,0:T(8,128)}, u32[]{:S(2)}) copy-start(f32[128,1024]{1,0:T(8,128)} %get-tuple-element.91) | copy-start | bytes 1572868
  295.4 4.4 %copy-start.4 = (f32[1024,128]{1,0:T(8,128)S(1)}, f32[1024,128]{1,0:T(8,128)}, u32[]{:S(2)}) copy-start(f32[1024,128]{1,0:T(8,128)} %get-tuple-element.92) | copy-start | bytes 1572868
  296.4 4.2 %copy-start.6 = (f32[512,128]{1,0:T(8,128)S(1)}, f32[512,128]{1,0:T(8,128)}, u32[]{:S(2)}) copy-start(f32[512,128]{1,0:T(8,128)} %get-tuple-element.93) | copy-start | bytes 786436
Sparse Core Ops, SparseCore 0:
  13.5 35.9 all-gather.3
  54.0 9.0 all-gather.5
  65.0 37.7 all-gather.7
where the time goes:
time: 308 us
  Pallas kernels  207 us (67%)
  waiting for transfers between devices  43.8 us (14%)
  local copies, waits for them, and re-layouts  31.1 us (10%)
  between operations  13.9 us (5%)
  matrix products  6.59 us (2%)
  other arithmetic  4.98 us (2%)
    pallas_call x1, Pallas kernels, middle(): pl.pallas_call(partial(middle_kernel, n), in_specs=[vmem] * 4 + [hbm] * 3...  93.2 us
    pallas_call x1, Pallas kernels, tail(): pl.pallas_call(partial(tail_kernel, n), in_specs=[vmem] * 13, out_specs=[...  50.9 us
    pallas_call x1, Pallas kernels, attend_back_scatter(): pl.pallas_call(partial(attend_back_scatter_kernel, scale=scale), grid=(pa...  41.4 us
    all_gather x1, waiting for transfers between devices, local(): pack = lax.all_gather(pack, BOTH, axis=0, tiled=True)  36.1 us
    pallas_call x1, Pallas kernels, attend(): pl.pallas_call(functools.partial(attend_kernel, scale=scale), grid=(S, pa...  21.7 us
    unnamed x45, local copies, waits for them, and re-layouts  14.4 us
    all_gather x1, waiting for transfers between devices, local(): lax.all_gather(jnp.concatenate([w_up, w_down.T], axis=1), BOTH, axis=0, t...  7.64 us
    dot_general x4, matrix products, dotf(): lax.dot_general(a, b, (((ca,), (cb,)), ((), ())), preferred_element_type=...  6.59 us
  transfers between devices with their start and end apart: 3, of which 2 were waited for; matrix products, arithmetic and copies ran while one was open for 6% of the time, Pallas kernels for 7%

commit v1 on v0

--- a/solution.py
+++ b/solution.py
@@ -18,7 +18,7 @@
     r=lax.broadcasted_iota(jnp.int32,(n,n),0); c=lax.broadcasted_iota(jnp.int32,(n,n),1)
     return (r+c==n-1).astype(F32).astype(dtype)
 
-def attend_kernel(q_ref,k_ref,v_ref,kd_ref,pq_ref,sq_ref,sk_ref,ctx_ref,p_ref,st_ref,*,scale):
+def attend_kernel(q_ref,k_ref,v_ref,kd_ref,pq_ref,sq_ref,sk_ref,ctx_ref,p_ref,st_ref,*,scale,between=None):
     rows=q_ref.shape[1]; total=k_ref.shape[1]; tile=min(TILE,rows)
     same_row=sk_ref[0]
     for half in range(2):
@@ -41,6 +41,8 @@
             p=e*(1.0/jnp.sum(e,axis=1,keepdims=True))
             p_ref[0,half,i0:i0+tile,:]=p
             ctx_ref[0,i0:i0+tile,cols]=dotf(p.astype(BF),v,1,0).astype(BF)
+        if between is not None:
+            between(half)
 
 def attend_back_kernel(q_ref,k_ref,v_ref,kd_ref,pq_ref,p_ref,dc_ref,dq_ref,dk_ref,dv_ref,dkd_ref,dpq_ref,ds_ref,pl_ref,dkt_ref,*,scale,between=None):
     rows=q_ref.shape[1]; total=k_ref.shape[1]; tile=min(TILE,rows)
@@ -262,9 +264,10 @@
     return rate * (scaled - jnp.mean(scaled, axis=1, keepdims=True) - unit * jnp.mean(scaled * unit, axis=1, keepdims=True))
 
 
-def middle_kernel(n, ctx, rows, wo_t, norms, cot_hbm, up_hbm, down_hbm, outputs, d_first, d_ctx, g_up, g_down, g_out, g_norm,
+def middle_kernel(n, ctx, rows, side, norms, cot_hbm, up_hbm, down_hbm, outputs, d_first, d_ctx, g_up, g_down, g_out, g_norm,
                   cot, up, down, low, act, d_ffn, d_hid, d_br, unit, slope, d_sec, rates, sums, load_sems, *line_refs):
     R, D = rows.shape
+    Wd = ctx.shape[1]
     chunk = R // (2 * ROUNDS)
     pair = 2 * chunk
     loads = [pltpu.make_async_copy(a, b, load_sems.at[i]) for i, (a, b) in
@@ -283,7 +286,7 @@
 
     def open_first(k):
         r = pair_rows(k)
-        lines[0].send[r, :] = dotf(ctx[r, :], wo_t[...], 1, 1).astype(BF)
+        lines[0].send[r, :] = dotf(ctx[r, :], side[:, :Wd], 1, 1).astype(BF)
 
     def first_to_second(k):
         r = pair_rows(k)
@@ -324,7 +327,7 @@
         d_first[r, :] = d1
         db = d1.astype(BF)
         d_br[r, :] = db
-        d_ctx[r, :] = dotf(db, wo_t[...], 1, 0).astype(BF)
+        d_ctx[r, :] = dotf(db, side[:, :Wd], 1, 0).astype(BF)
 
     def weight_grad(out, left, right):
         width = min(256, D)
@@ -390,9 +393,9 @@
     lax.fori_loop(0, ROUNDS, finish, 0)
 
 
-def middle(n, ctx, rows, wo_t, norms, cot, up, down):
+def middle(n, ctx, rows, side, norms, cot, up, down):
     R, D = rows.shape
-    Wd, F = wo_t.shape[1], up.shape[1]
+    Wd, F = ctx.shape[1], up.shape[1]
     vmem, hbm = pl.BlockSpec(memory_space=pltpu.VMEM), pl.BlockSpec(memory_space=pl.ANY)
     line = [pltpu.VMEM((R, D), BF)] * 4 + [pltpu.SemaphoreType.DMA((6, 2, ROUNDS))]
     shape = jax.ShapeDtypeStruct
@@ -409,7 +412,7 @@
         compiler_params=pltpu.CompilerParams(collective_id=1, has_side_effects=True),
         name="middle",
         cost_estimate=pl.CostEstimate(flops=12 * R * D * F, bytes_accessed=16 * R * D, transcendentals=2 * R * F),
-    )(ctx, rows, wo_t, norms, cot, up, down)
+    )(ctx, rows, side, norms, cot, up, down)
 
 
 def plane_peers():
@@ -569,11 +572,11 @@
     )(q, k, v, kd, pq, p, dc, g_up, g_down)
 
 
-def tail_kernel(n, dq, dk, dv, wqkv, rows, d_first, pos_t, to_row, from_row, dkd, dpq, g_out, g_norm,
+def tail_kernel(n, dq, dk, dv, wqkv, rows, d_first, side, to_row, from_row, dkd, dpq, g_out, g_norm,
                 grad_in, o_q, o_k, o_v, o_out, o_pos, o_norm,
                 k_in, v_in, dqkv, d_pos, g_left, g_right, norm_in, swap_sems, norm_sems, *refs):
     L, Wd = dq.shape
-    D, B = pos_t.shape
+    D, B = side.shape[0], side.shape[1] - Wd
     W = to_row.shape[1]
     own = D // 8
     chunk = L // (2 * ROUNDS)
@@ -659,7 +662,7 @@
     def left_tile(i, _):
         r = pl.ds(pl.multiple_of(i * width, width), width)
         g = dotf(rows[:, r], dqkv[...], 0, 0)
-        g_left[r, :2 * Wd] = (g[:, :2 * Wd] + dotf(pos_t[r, :], d_pos[...], 1, 0)).astype(BF)
+        g_left[r, :2 * Wd] = (g[:, :2 * Wd] + dotf(side[r, Wd:], d_pos[...], 1, 0)).astype(BF)
         g_left[r, 2 * Wd:] = g[:, 2 * Wd:].astype(BF)
         return 0
     lax.fori_loop(0, D // width, left_tile, 0)
@@ -731,9 +734,9 @@
         copy.wait_send()
 
 
-def tail(n, dq, dk, dv, wqkv, rows, d_first, pos_t, to_row, from_row, dkd, dpq, g_out, g_norm):
+def tail(n, dq, dk, dv, wqkv, rows, d_first, side, to_row, from_row, dkd, dpq, g_out, g_norm):
     L, Wd = dq.shape
-    D, B = pos_t.shape
+    D, B = side.shape[0], side.shape[1] - Wd
     own = D // 8
     vmem = pl.BlockSpec(memory_space=pltpu.VMEM)
     shape = jax.ShapeDtypeStruct
@@ -750,7 +753,216 @@
         compiler_params=pltpu.CompilerParams(collective_id=4, has_side_effects=True),
         name="tail",
         cost_estimate=pl.CostEstimate(flops=8 * L * D * 3 * Wd, bytes_accessed=16 * L * D, transcendentals=0),
-    )(dq, dk, dv, wqkv, rows, d_first, pos_t, to_row, from_row, dkd, dpq, g_out, g_norm)
+    )(dq, dk, dv, wqkv, rows, d_first, side, to_row, from_row, dkd, dpq, g_out, g_norm)
+
+
+class Gather:
+    def __init__(self, mats, sems, first=None):
+        self.mats, self.sems, self.first = mats, sems, first
+        self.near, self.core = plane_peers()
+        self.own = mats[0].shape[0] // 8
+
+    def rows(self, j, other=False):
+        core = 1 - self.core if other else self.core
+        return pl.ds(pl.multiple_of((2 * self.near[j] + core) * self.own, self.own), self.own)
+
+    def copy(self, side, rows, kind, i, device, first=False):
+        block = self.mats[side].at[rows, :]
+        return pltpu.make_async_remote_copy(
+            src_ref=self.first[side] if first and self.first is not None else block, dst_ref=block,
+            send_sem=self.sems.at[0, kind, side, i], recv_sem=self.sems.at[1, kind, side, i], device_id=device, device_id_type=MESH)
+
+    def direct(self, side, axis, receive=False):
+        return self.copy(side, self.rows(axis if receive else 0), 0, axis, {"shard": self.near[axis]}, not receive)
+
+    def relay(self, side, receive=False):
+        return self.copy(side, self.rows(3 if receive else 1 + side), 0, 0, {"shard": self.near[2 - side]})
+
+    def partner(self, side, j, receive=False):
+        return self.copy(side, self.rows(j, receive), 1, j, {"context": 1 - self.core}, j == 0 and not receive)
+
+    def begin(self):
+        for a in (0, 1):
+            self.direct(a, 1 + a).start()
+        for a in (0, 1):
+            self.direct(a, 2 - a).start()
+        for a in (0, 1):
+            self.partner(a, 0).start()
+
+    def turn(self):
+        for a in (0, 1):
+            self.direct(a, 1 + a, True).wait_recv()
+            self.relay(a).start()
+            self.partner(a, 1 + a).start()
+
+    def share(self):
+        for a in (0, 1):
+            self.direct(a, 2 - a, True).wait_recv()
+            self.partner(a, 2 - a).start()
+
+    def corner(self):
+        for a in (0, 1):
+            self.relay(a, True).wait_recv()
+            self.partner(a, 3).start()
+
+    def close(self):
+        for a in (0, 1):
+            for j in range(4):
+                self.partner(a, j, True).wait_recv()
+        for a in (0, 1):
+            self.direct(a, 1).wait_send()
+            self.direct(a, 2).wait_send()
+            self.relay(a).wait_send()
+            for j in range(4):
+                self.partner(a, j).wait_send()
+
+
+def open_kernel(x, w_q, w_k, w_v, w_o, pos, norms, to_row, from_row, q, k, v, kd, pq, wqkv, side, all_norms,
+                x_in, pos_qk, swap_sems, norm_sems, sems):
+    L, D = x.shape
+    own, Wd = w_q.shape
+    B, W = pos.shape[0], to_row.shape[1]
+    near, c = plane_peers()
+    mine = pl.ds(pl.multiple_of((2 * near[0] + c) * own, own), own)
+    wqkv[mine, :Wd] = w_q[...]
+    wqkv[mine, Wd:2 * Wd] = w_k[...]
+    wqkv[mine, 2 * Wd:] = w_v[...]
+    side[mine, :Wd] = w_o[...].T
+    side[mine, Wd:] = pos[...].T
+    all_norms[:, mine] = norms[...]
+    peers = [(j, other) for j in range(4) for other in (0, 1) if j or other]
+    device = lambda j, other: {"shard": near[j], "context": 1 - c if other else c}
+    barrier = pltpu.get_barrier_semaphore()
+    for j, other in peers:
+        pl.semaphore_signal(barrier, inc=1, device_id=device(j, other), device_id_type=MESH)
+    pl.semaphore_wait(barrier, 7)
+    job = Gather((wqkv, side), sems)
+    job.begin()
+    swap = pltpu.make_async_remote_copy(src_ref=x, dst_ref=x_in, send_sem=swap_sems.at[0], recv_sem=swap_sems.at[1],
+                                        device_id={"context": 1 - c}, device_id_type=MESH)
+    swap.start()
+
+    def piece(j, other, receive):
+        core = 1 - c if other and receive else c
+        lanes = pl.ds(pl.multiple_of((2 * near[j if receive else 0] + core) * own, own), own)
+        return pltpu.make_async_remote_copy(
+            src_ref=norms, dst_ref=all_norms.at[:, lanes], send_sem=norm_sems.at[0, 2 * j + other],
+            recv_sem=norm_sems.at[1, 2 * j + other], device_id=device(j, other), device_id_type=MESH)
+    for j, other in peers:
+        piece(j, other, False).start()
+    job.turn()
+    job.share()
+    swap.wait_recv()
+    job.corner()
+    job.close()
+    tile = min(256, L)
+
+    def project(i, _):
+        r = pl.ds(pl.multiple_of(i * tile, tile), tile)
+        here = pl.ds(pl.multiple_of(c * L + i * tile, tile), tile)
+        there = pl.ds(pl.multiple_of((1 - c) * L + i * tile, tile), tile)
+        out = dotf(x[r, :], wqkv[...], 1, 0).astype(BF)
+        q[r, :] = out[:, :Wd]
+        k[here, :] = out[:, Wd:2 * Wd]
+        v[here, :] = out[:, 2 * Wd:]
+        out = dotf(x_in[r, :], wqkv[:, Wd:], 1, 0).astype(BF)
+        k[there, :] = out[:, :Wd]
+        v[there, :] = out[:, Wd:]
+        return 0
+    lax.fori_loop(0, L // tile, project, 0)
+    pos_qk[...] = dotf(side[:, Wd:], wqkv[:, :2 * Wd], 0, 0).astype(BF)
+    ids = lax.broadcasted_iota(jnp.int32, (B, 256), 0)
+
+    def table(i, _):
+        r = pl.ds(pl.multiple_of(i * 256, 256), 256)
+        kd[r, :] = dotf((ids == to_row[:, r]).astype(F32).astype(BF), pos_qk[:, Wd:], 0, 0).astype(BF)
+        pq[r, :] = dotf((ids == from_row[:, r]).astype(F32).astype(BF), pos_qk[:, :Wd], 0, 0).astype(BF)
+        return 0
+    lax.fori_loop(0, W // 256, table, 0)
+    for j, other in peers:
+        piece(j, other, True).wait_recv()
+    for j, other in peers:
+        piece(j, other, False).wait_send()
+    swap.wait_send()
+
+
+def open_gather(x, w_q, w_k, w_v, w_o, pos, norms, to_row, from_row):
+    L, D = x.shape
+    own, Wd = w_q.shape
+    B, W = pos.shape[0], to_row.shape[1]
+    T = W - L
+    vmem = pl.BlockSpec(memory_space=pltpu.VMEM)
+    shape = jax.ShapeDtypeStruct
+    return pl.pallas_call(
+        open_kernel, in_specs=[vmem] * 9, out_specs=[vmem] * 8,
+        out_shape=[shape((L, Wd), BF), shape((T, Wd), BF), shape((T, Wd), BF), shape((W, Wd), BF), shape((W, Wd), BF),
+                   shape((D, 3 * Wd), BF), shape((D, Wd + B), BF), shape((8, D), F32)],
+        scratch_shapes=[pltpu.VMEM((L, D), BF), pltpu.VMEM((B, 2 * Wd), BF), pltpu.SemaphoreType.DMA((2,)),
+                        pltpu.SemaphoreType.DMA((2, 8)), pltpu.SemaphoreType.DMA((2, 2, 2, 4))],
+        compiler_params=pltpu.CompilerParams(collective_id=5, has_side_effects=True),
+        name="open",
+        cost_estimate=pl.CostEstimate(flops=10 * L * D * Wd, bytes_accessed=8 * L * D, transcendentals=0),
+    )(x, w_q, w_k, w_v, w_o, pos, norms, to_row, from_row)
+
+
+def attend_gather_kernel(*refs, scale):
+    ins, (w_up, w_down), outs, mats, st, turned, sems, local_sems = refs[:7], refs[7:9], refs[9:11], refs[11:13], *refs[13:]
+    step, last = pl.program_id(1), pl.num_programs(1) - 1
+    job = Gather(mats, sems, first=(w_up, turned))
+    keep = [pltpu.make_async_copy(a, m.at[job.rows(0), :], local_sems.at[i])
+            for i, (a, m) in enumerate(zip((w_up, turned), mats))]
+
+    @pl.when(step == 0)
+    def _():
+        turned[...] = w_down[...].T
+        greet_plane()
+        job.begin()
+        for copy in keep:
+            copy.start()
+
+    def between(half):
+        if half == 1:
+            @pl.when(step == 0)
+            def _():
+                job.turn()
+        else:
+            @pl.when(step == last)
+            def _():
+                job.share()
+
+    attend_kernel(*ins, *outs, st, scale=scale, between=between)
+
+    @pl.when(step == last)
+    def _():
+        job.corner()
+        job.close()
+        for copy in keep:
+            copy.wait()
+
+
+def attend_gather(q, k, v, kd, pq, sq, sk, w_up, w_down, scale):
+    S, L, Wd = q.shape
+    T = k.shape[1]
+    W = kd.shape[0]
+    own, F = w_up.shape
+    pairs = Wd // 128
+    row = lambda n: pl.BlockSpec((1, n, 128), lambda s, h: (s, 0, h))
+    tab = pl.BlockSpec((W, 128), lambda s, h: (0, h))
+    vmem, hbm = pl.BlockSpec(memory_space=pltpu.VMEM), pl.BlockSpec(memory_space=pl.ANY)
+    shape = jax.ShapeDtypeStruct
+    return pl.pallas_call(
+        partial(attend_gather_kernel, scale=scale), grid=(S, pairs),
+        in_specs=[row(L), row(T), row(T), tab, tab, pl.BlockSpec((1, L, 1), lambda s, h: (s, 0, 0)),
+                  pl.BlockSpec((1, 1, T), lambda s, h: (s, 0, 0)), vmem, vmem],
+        out_specs=[row(L), pl.BlockSpec((1, 2, L, T), lambda s, h: (s, h, 0, 0)), hbm, hbm],
+        out_shape=[shape((S, L, Wd), BF), shape((S, Wd // HD, L, T), F32), shape((8 * own, F), BF), shape((8 * own, F), BF)],
+        scratch_shapes=[pltpu.VMEM((L, T), F32), pltpu.VMEM((own, F), BF), pltpu.SemaphoreType.DMA((2, 2, 2, 4)),
+                        pltpu.SemaphoreType.DMA((2,))],
+        compiler_params=pltpu.CompilerParams(collective_id=6, has_side_effects=True),
+        name="attend",
+        cost_estimate=pl.CostEstimate(flops=int(16 * S * L * T * Wd), bytes_accessed=int(S * L * T * Wd // HD * 4),
+                                      transcendentals=S * L * T * Wd // HD),
+    )(q, k, v, kd, pq, sq, sk, w_up, w_down)
 
 
 def split_columns(packed, widths):
@@ -772,54 +984,60 @@
     first = lax.axis_index("context") * L
     W = T + L
     own = w_query.shape[0]
-    norms = jnp.stack([gain_attn, bias_attn, gain_ffn, bias_ffn], axis=1)
-    norms = jnp.pad(norms, ((0, 0), (0, 124)))
-    pack = jnp.concatenate([w_query, w_key, w_value, w_output.T, positions.T, norms], axis=1)
-    pack = lax.all_gather(pack, BOTH, axis=0, tiled=True)
-    wq, wk, wv, wo_t, pos_t, norms = split_columns(pack, (Wd, Wd, Wd, Wd, B, 128))
-    ffn = lax.all_gather(jnp.concatenate([w_up, w_down.T], axis=1), BOTH, axis=0, tiled=True)
-    up, down_t = split_columns(ffn, (F, F))
-    norms = jnp.pad(norms[:, :4].astype(F32).T, ((0, 4), (0, 0)))
-    rows = inputs.reshape(S * L, D)
-    wqkv = pack[:, :3 * Wd]
-    qkv = dotf(rows, wqkv, 1, 0).astype(BF)
-    q, k, v = [x.reshape(S, L, Wd) for x in split_columns(qkv, (Wd, Wd, Wd))]
-    k, v = split_last(lax.all_gather(jnp.concatenate([k, v], axis=2), "context", axis=1, tiled=True), Wd)
-    pos_qk = dotf(pos_t, jnp.concatenate([wq, wk], axis=1), 0, 0).astype(BF)
     flipped = jnp.concatenate([buckets[::-1], buckets[:1]])
     to = lax.dynamic_slice_in_dim(flipped, T - L - first, W, 0)
     fro = lax.dynamic_slice_in_dim(flipped, first, W, 0)
-    ids = jnp.arange(B, dtype=jnp.int32)
-    pick_to = (to[:, None] == ids[None]).astype(BF)
-    pick_from = (fro[:, None] == ids[None]).astype(BF)
-    kd = dotf(pick_to, pos_qk[:, Wd:], 1, 0).astype(BF)
-    pq = dotf(pick_from, pos_qk[:, :Wd], 1, 0).astype(BF)
     seg_here = lax.dynamic_slice_in_dim(segments, first, L, 1)[:, :, None]
-    ctx, probs = attend(q, k, v, kd, pq, seg_here, segments[:, None, :], scale)
+    seg_row = segments[:, None, :]
+    rows = inputs.reshape(S * L, D)
+    square = (lax.axis_size("shard"), lax.axis_size("context"), S, own * 8, 3 * Wd) == (4, 2, 1, D, Wd + B)
+    norms = jnp.stack([gain_attn, bias_attn, gain_ffn, bias_ffn]).astype(F32)
+    if square:
+        q, k, v, kd, pq, wqkv, side, norms = open_gather(
+            rows, w_query, w_key, w_value, w_output, positions, jnp.pad(norms, ((0, 4), (0, 0))), to[None], fro[None])
+        q, k, v = q[None], k[None], v[None]
+        ctx, probs, up, down_t = attend_gather(q, k, v, kd, pq, seg_here, seg_row, w_up, w_down, scale)
+    else:
+        norms = jnp.pad(norms.astype(BF).T, ((0, 0), (0, 124)))
+        pack = jnp.concatenate([w_query, w_key, w_value, w_output.T, positions.T, norms], axis=1)
+        pack = lax.all_gather(pack, BOTH, axis=0, tiled=True)
+        wqkv, side, norms = split_columns(pack, (3 * Wd, Wd + B, 128))
+        ffn = lax.all_gather(jnp.concatenate([w_up, w_down.T], axis=1), BOTH, axis=0, tiled=True)
+        up, down_t = split_columns(ffn, (F, F))
+        norms = jnp.pad(norms[:, :4].astype(F32).T, ((0, 4), (0, 0)))
+        qkv = dotf(rows, wqkv, 1, 0).astype(BF)
+        q, k, v = [x.reshape(S, L, Wd) for x in split_columns(qkv, (Wd, Wd, Wd))]
+        k, v = split_last(lax.all_gather(jnp.concatenate([k, v], axis=2), "context", axis=1, tiled=True), Wd)
+        pos_qk = dotf(side[:, Wd:], wqkv[:, :2 * Wd], 0, 0).astype(BF)
+        ids = jnp.arange(B, dtype=jnp.int32)
+        pick_to = (to[:, None] == ids[None]).astype(BF)
+        pick_from = (fro[:, None] == ids[None]).astype(BF)
+        kd = dotf(pick_to, pos_qk[:, Wd:], 1, 0).astype(BF)
+        pq = dotf(pick_from, pos_qk[:, :Wd], 1, 0).astype(BF)
+        ctx, probs = attend(q, k, v, kd, pq, seg_here, seg_row, scale)
     ctx_rows = ctx.reshape(S * L, Wd)
     outputs, d_first, d_ctx, g_up, g_down_t, g_out_t, g_norm = middle(
-        lax.axis_size("tensor"), ctx_rows, rows, wo_t, norms, cotangent.reshape(S * L, D), up, down_t)
+        lax.axis_size("tensor"), ctx_rows, rows, side, norms, cotangent.reshape(S * L, D), up, down_t)
     outputs = outputs.reshape(inputs.shape)
     f = lambda x: x.astype(F32)
-    if (lax.axis_size("shard"), lax.axis_size("context"), S, own * 8, 3 * Wd) == (4, 2, 1, D, Wd + B):
+    if square:
         dq, dk, dv, dkd, dpq, g_up, g_down = attend_back_scatter(q, k, v, kd, pq, probs, d_ctx.reshape(S, L, Wd), g_up, g_down_t, scale)
         grad_inputs, g_q, g_k, g_v, g_o, g_p, g_n = tail(
-            lax.axis_size("tensor"), dq[0], dk[0], dv[0], wqkv, rows, d_first, pos_t, to[None], fro[None], dkd, dpq, g_out_t, g_norm)
+            lax.axis_size("tensor"), dq[0], dk[0], dv[0], wqkv, rows, d_first, side, to[None], fro[None], dkd, dpq, g_out_t, g_norm)
         return (outputs, grad_inputs.reshape(inputs.shape), g_q, g_k, g_v, g_o, g_up, g_down, g_p, g_n[0], g_n[1], g_n[2], g_n[3])
     scatter = partial(lax.psum_scatter, axis_name=BOTH, scatter_dimension=0, tiled=True)
     g_ffn = scatter(jnp.concatenate([g_up, g_down_t], axis=1))
     dq, dk, dv, dkd, dpq = attend_back(q, k, v, kd, pq, probs, d_ctx.reshape(S, L, Wd), scale)
     dkv = lax.psum_scatter(jnp.concatenate([dk, dv], axis=2), "context", scatter_dimension=1, tiled=True)
     dqkv = jnp.concatenate([dq, dkv], axis=2).reshape(S * L, 3 * Wd)
-    weights = jnp.concatenate([wq, wk, wv], axis=1)
-    d_in = lax.psum(dotf(dqkv, weights, 1, 1).astype(BF), "tensor").astype(F32)
+    d_in = lax.psum(dotf(dqkv, wqkv, 1, 1).astype(BF), "tensor").astype(F32)
     grad_inputs = (d_first + d_in).astype(BF).reshape(inputs.shape)
     d_pos_key = dotf(pick_to, dkd.astype(BF), 0, 0)
     d_pos_query = dotf(pick_from, dpq.astype(BF), 0, 0)
     d_pos = jnp.concatenate([d_pos_query, d_pos_key], axis=1).astype(BF)
     g_qkv = dotf(rows, dqkv, 0, 0)
-    g_pos_t = dotf(jnp.concatenate([wq, wk], axis=1), d_pos, 1, 1)
-    g_qk = g_qkv[:, :2 * Wd] + dotf(pos_t, d_pos, 1, 0)
+    g_pos_t = dotf(wqkv[:, :2 * Wd], d_pos, 1, 1)
+    g_qk = g_qkv[:, :2 * Wd] + dotf(side[:, Wd:], d_pos, 1, 0)
     g_norm = jnp.pad(g_norm.T, ((0, 0), (0, 120)))
     pack = jnp.concatenate([x.astype(BF) for x in (g_qk, g_qkv[:, 2 * Wd:], g_out_t, g_pos_t, g_norm)], axis=1)
     g_q, g_k, g_v, g_o, g_p, g_n = split_columns(scatter(pack), (Wd, Wd, Wd, Wd, B, 128))

time: 308 us -> 258 us (0.84)
  waiting for transfers between devices: 43.8 us -> 0 us
  Pallas kernels: 207 us -> 242 us
  local copies, waits for them, and re-layouts: 31.1 us -> 13 us
  between operations: 13.9 us -> 0.75 us
  matrix products: 6.59 us -> 0 us
    all_gather x3 -> x0, waiting for transfers between devices: 43.8 us -> none  [the longest x1 36.1 us: local(): pack = lax.all_gather(pack, BOTH, axis=0, tiled=True)]
    pallas_call x1 -> x2, Pallas kernels: 21.7 us -> 55.1 us  [the longest x1 28.9 us: open_gather(): pl.pallas_call(open_kernel, in_specs=[vmem] * 9, out_specs=[vmem] * 8, ou...]
    slice x5 -> x0, local copies, waits for them, and re-layouts: 10 us -> none  [the longest x3 6.53 us: split_columns(): out.append(packed[:, at:at + width])]
    unnamed x45 -> x29, local copies, waits for them, and re-layouts: 14.4 us -> 7.73 us
    dot_general x4 -> x0, matrix products: 6.59 us -> none  [dotf(): lax.dot_general(a, b, (((ca,), (cb,)), ((), ())), preferred_element_type=...]
  transfers between devices with their start and end apart: 3 -> 0, of which waited for: 2 -> 0; matrix products, arithmetic and copies ran while one was open for 6% -> 0% of each run, Pallas kernels for 7% -> 0%
where the time goes in v1:
time: 258 us
  Pallas kernels  242 us (94%)
  local copies, waits for them, and re-layouts  13 us (5%)
    pallas_call x1, Pallas kernels, middle(): pl.pallas_call(partial(middle_kernel, n), in_specs=[vmem] * 4 + [hbm] * 3...  94.1 us
    pallas_call x1, Pallas kernels, tail(): pl.pallas_call(partial(tail_kernel, n), in_specs=[vmem] * 13, out_specs=[...  51.1 us
    pallas_call x1, Pallas kernels, attend_back_scatter(): pl.pallas_call(partial(attend_back_scatter_kernel, scale=scale), grid=(pa...  41.4 us
    pallas_call x1, Pallas kernels, open_gather(): pl.pallas_call(open_kernel, in_specs=[vmem] * 9, out_specs=[vmem] * 8, ou...  28.9 us
    pallas_call x1, Pallas kernels, attend_gather(): pl.pallas_call(partial(attend_gather_kernel, scale=scale), grid=(S, pairs...  26.2 us
    unnamed x29, local copies, waits for them, and re-layouts  7.73 us

profile of v1, /device:TPU:0, one launch (start us, length us, event | category | flops | bytes accessed | tf_op | source)
XLA Modules:
  0.0 257.5 jit_solution(8101946503596562105)
XLA Ops:
  0.6 1.2 slice.15
  1.8 0.7 dynamic-slice_bitcast_fusion
  2.5 1.3 fusion.7.norms
  3.8 0.8 reverse
  4.6 0.1 slice.24
  4.7 0.7 dynamic-slice_add_fusion
  5.4 0.6 broadcast_in_dim.24.from_row
  6.0 0.6 broadcast_in_dim.23.to_row
  6.6 0.9 copy.28.refs_5_
  7.5 28.9 %open.1 = (bf16[512,256]{1,0:T(8,128)(2,1)}, bf16[1024,256]{1,0:T(8,128)(2,1)}, bf16[1024,256]{1,0:T(8,128)(2,1)}, bf16[1536,256]{1,0:T(8,128)(2,1)}, bf16[1536,...) custom-call(bf16[512,1024]{1,0:T(8,128)(2,1)} %bitcast.37, ...), custom_call_target="tpu_custom_call" | custom-call | flops 1342177280 | bytes 4194304 | tf_op jit(solution)/shard_map/open/pallas_call | solution.py:896
  36.4 26.2 %attend.1 = (bf16[1,512,256]{2,1,0:T(8,128)(2,1)}, f32[1,4,512,1024]{3,2,1,0:T(8,128)}, bf16[1024,1024]{1,0:T(8,128)(2,1)}, bf16[1024,1024]{1,0:T(8,128)(2,1)}) custom-call(bf16[1,512,256]{2,1,0:T(8,128)(2,1)} %bitcast.46, bf16[1,1024,256]{2,1,0:T(8,128)(2,1)} %bitcast.40, bf16[1,1024,256]{2,1,0:T(8,128)(2,1)} %bitcast.42, ...), custom_call_target="tpu_custom_call" | custom-call | flops 2147483648 | bytes 8388608 | tf_op jit(solution)/shard_map/attend/pallas_call | solution.py:953
  62.6 94.1 %middle.1 = (bf16[512,1024]{1,0:T(8,128)(2,1)}, f32[512,1024]{1,0:T(8,128)}, bf16[512,256]{1,0:T(8,128)(2,1)}, bf16[1024,1024]{1,0:T(8,128)(2,1)}, bf16[1024,102...) custom-call(bf16[512,256]{1,0:T(8,128)(2,1)} %bitcast.50, bf16[512,1024]{1,0:T(8,128)(2,1)} %bitcast.38, ...), custom_call_target="tpu_custom_call" | custom-call | flops 6442450944 | bytes 8388608 | tf_op jit(solution)/shard_map/middle/pallas_call | solution.py:402
  156.7 41.4 %attend_back.1 = (bf16[1,512,256]{2,1,0:T(8,128)(2,1)}, bf16[1,1024,256]{2,1,0:T(8,128)(2,1)}, bf16[1,1024,256]{2,1,0:T(8,128)(2,1)}, f32[1536,256]{1,0:T(8,128)...) custom-call(bf16[1,512,256]{2,1,0:T(8,128)(2,1)} %bitcast.47, bf16[1,1024,256]{2,1,0:T(8,128)(2,1)} %bitcast.41, ...), custom_call_target="tpu_custom_call" | custom-call | flops 4294967296 | bytes 8388608 | tf_op jit(solution)/shard_map/attend_back/pallas_call | solution.py:562
  198.1 0.0 copy-start
  198.1 51.1 %tail.1 = (bf16[512,1024]{1,0:T(8,128)(2,1)}, f32[128,256]{1,0:T(8,128)}, f32[128,256]{1,0:T(8,128)}, f32[128,256]{1,0:T(8,128)}, f32[256,128]{1,0:T(8,128)}, /*index=5*/f32[512,128]{1,0:T(8,128)}, f32[8,128]{1,0:T(8,128)}) custom-call(bf16[512,256]{1,0:T(8,128)(2,1)} %bitcast.48, bf16[1024,256]{1,0:T(8,128)(2,1)} %bitcast.44, bf16[1024,256]{1,0:T(8,128)(2,1)} %bitcast.45, ...), custom_call_target="tpu_custom_call" | custom-call | flops 3221225472 | bytes 8388608 | tf_op jit(solution)/shard_map/tail/pallas_call | solution.py:745
  249.2 0.0 copy-start.1
  249.3 1.4 slice_bitcast_fusion
  250.6 0.0 copy-done
  250.6 0.0 copy-start.8
  250.6 0.0 copy-start.7
  250.6 0.0 copy-start.6
  250.6 0.0 copy-start.5
  250.6 1.0 copy.38
  251.6 0.0 copy-done.1
  251.6 0.0 copy-start.3
  251.6 0.0 copy-start.2
  251.6 1.0 copy.39
  252.6 0.0 copy-done.8
  252.6 0.0 copy-start.4
  252.6 0.7 copy.40
  253.3 0.0 copy-done.7
  253.3 0.7 copy.41
  253.9 0.0 copy-done.6
  253.9 0.7 copy.42
  254.6 0.0 copy-done.5
  254.6 0.7 copy.43
  255.2 0.0 copy-done.3
  255.2 0.8 copy.44
  256.0 0.0 copy-done.2
  256.0 0.8 copy.45
  256.8 0.0 copy-done.4
  256.8 0.7 copy.46
Async XLA Ops:
  198.1 52.5 %copy-start = (bf16[512,1024]{1,0:T(8,128)(2,1)S(1)}, bf16[512,1024]{1,0:T(8,128)(2,1)}, u32[]{:S(2)}) copy-start(bf16[512,1024]{1,0:T(8,128)(2,1)} %get-tuple-element.56) | copy-start | bytes 3145732
  249.2 2.4 copy-start.1
  250.6 2.0 copy-start.8
  250.6 2.6 %copy-start.7 = (f32[128,256]{1,0:T(8,128)S(1)}, f32[128,256]{1,0:T(8,128)}, u32[]{:S(2)}) copy-start(f32[128,256]{1,0:T(8,128)} %get-tuple-element.101) | copy-start | bytes 393220
  250.6 3.3 %copy-start.6 = (f32[128,256]{1,0:T(8,128)S(1)}, f32[128,256]{1,0:T(8,128)}, u32[]{:S(2)}) copy-start(f32[128,256]{1,0:T(8,128)} %get-tuple-element.102) | copy-start | bytes 393220
  250.6 3.9 %copy-start.5 = (f32[256,128]{1,0:T(8,128)S(1)}, f32[256,128]{1,0:T(8,128)}, u32[]{:S(2)}) copy-start(f32[256,128]{1,0:T(8,128)} %get-tuple-element.103) | copy-start | bytes 393220
  251.6 3.6 %copy-start.3 = (f32[128,1024]{1,0:T(8,128)S(1)}, f32[128,1024]{1,0:T(8,128)}, u32[]{:S(2)}) copy-start(f32[128,1024]{1,0:T(8,128)} %get-tuple-element.104) | copy-start | bytes 1572868
  251.6 4.4 %copy-start.2 = (f32[1024,128]{1,0:T(8,128)S(1)}, f32[1024,128]{1,0:T(8,128)}, u32[]{:S(2)}) copy-start(f32[1024,128]{1,0:T(8,128)} %get-tuple-element.105) | copy-start | bytes 1572868
  252.6 4.2 %copy-start.4 = (f32[512,128]{1,0:T(8,128)S(1)}, f32[512,128]{1,0:T(8,128)}, u32[]{:S(2)}) copy-start(f32[512,128]{1,0:T(8,128)} %get-tuple-element.106) | copy-start | bytes 786436
